TPU v7x, 256 devices: a whole 4x4x8 slice. The times are simulated.
256 devices in a mesh: tm: 128 (over z, y, x), tensor: 2 (over core).
Axes of the slice: x: 4, y: 4, z: 8, core: 2. Of those that a mesh axis runs over, the one named last changes fastest.
Arguments:
- noise_start: float32 [1, 16384], replicated, may hold values from -6 to 6
- timesteps: int32 [129], replicated, may hold values from 0 to 599, as said below
- class_labels: int32 [128, 1], P('tm'), may hold values from 0 to 999
- mixing: float32 [2, 128], P(None, 'tm'), may hold values from -0.5 to 0.5
- class_table: bfloat16 [1000, 768], replicated, may hold values from -3 to 3
- time_in: bfloat16 [256, 768], replicated, may hold values from -0.75 to 0.75
- time_out: bfloat16 [768, 768], replicated, may hold values from -0.21875 to 0.21875
- ada_weight: bfloat16 [768, 4608], replicated, may hold values from -0.21875 to 0.21875
- final_ada: bfloat16 [768, 1536], replicated, may hold values from -0.21875 to 0.21875
- patch_weight: bfloat16 [16, 768], replicated, may hold values from -1.5 to 1.5
- q_weight: bfloat16 [768, 768], replicated, may hold values from -1.5 to 1.5
- kv_weight: bfloat16 [768, 1536], replicated, may hold values from -1.5 to 1.5
- out_weight: bfloat16 [768, 768], replicated, may hold values from -0.4375 to 0.4375
- up_weight: bfloat16 [768, 3072], P(None, 'tensor'), may hold values from -0.21875 to 0.21875
- down_weight: bfloat16 [3072, 768], P('tensor'), may hold values from -0.21875 to 0.21875
- final_weight: bfloat16 [768, 16], replicated, may hold values from -0.21875 to 0.21875
Outputs:
- states: float32 [128, 1, 16384], P('tm')
- residuals: float32 [2, 128], P(None, 'tm')
Inputs may be any that keep to these rules, and one draw needn't show every extreme that they name: `timesteps`: strictly decreasing; the first is 599, the last is 0, all others lie from 100 to 549.
All inputs are finite; a program needn't handle non-finite values.
Results may differ from a plain program's by a relative error of at most 0.008.
Values may be sent and summed in bfloat16 or wider, within the bound.
No kernel may reach another device: no remote copies, remote signals or barrier semaphores. Data moves between devices by JAX's collectives and lax.ppermute only.
A program may use at most 128 MiB of HBM per device.

v0:
```python
import math

import jax
import jax.numpy as jnp
import numpy as np
from jax import lax
from jax.experimental import pallas as pl
from jax.experimental.pallas import tpu as pltpu
from jax.sharding import Mesh
from jax.sharding import PartitionSpec as P

D = 768
HEADS = 12
SEQ = 1024
PATCH = 16
FREQ = 256
ITERS = 2
FF_OWN = 1536
TM = ("tm_0", "tm_1", "tm_2")
PLANE = ("tm_1", "tm_2")

norm_eps = 1e-06
plan_steps = 1000

OWN = SEQ // 2
LANES = 128
PER_ROW = LANES // PATCH
DENSE = OWN // PER_ROW
HALF = D // 2
ROWS = 256
GROUPS = ROWS // DENSE
MIB = 1 << 20
EXTRA = 8
FULL = DENSE + EXTRA
STEP = 32
PAIRS = HEADS // 2
Q_FACTOR = math.log2(math.e) / math.sqrt(D // HEADS)


def log_table():
    levels = np.arange(plan_steps, dtype=np.float64)
    beta_values = 0.0001 + (0.02 - 0.0001) * levels / (plan_steps - 1)
    table = np.zeros((8, LANES), np.float32)
    table.reshape(-1)[:plan_steps] = np.cumsum(np.log(1.0 - beta_values))
    return table


def angle_table(width, steps, first):
    rates = np.exp(-math.log(10000.0) * np.arange(width, dtype=np.float64) / width)
    angles = np.asarray(steps, np.float64)[:, None] * rates[None, :]
    parts = [np.cos(angles), np.sin(angles)]
    if first == "sin":
        parts = parts[::-1]
    return np.concatenate(parts, axis=1).astype(np.float32)


def place_tables():
    coarse = angle_table(HALF, PER_ROW * np.arange(SEQ // PER_ROW), "sin")
    return coarse, angle_table(HALF, np.arange(PER_ROW), "sin")


def time_table():
    count = np.arange(STEP)
    return np.concatenate(
        [angle_table(FREQ // 2, STEP * count, "cos"), angle_table(FREQ // 2, count, "cos")]
    )


def normed(values, shift, scale):
    center = values - jnp.mean(values, axis=-1, keepdims=True)
    spread = jnp.mean(center * center, axis=-1, keepdims=True)
    return center * lax.rsqrt(spread + norm_eps) * (1.0 + scale) + shift


def matmul(a, b):
    return jnp.dot(a, b, preferred_element_type=jnp.float32)


VMEM = pl.BlockSpec(memory_space=pltpu.VMEM)
SMEM = pl.BlockSpec(memory_space=pltpu.SMEM)
HBM = pl.BlockSpec(memory_space=pltpu.HBM)


def condition_kernel(
    where_ref,
    timesteps_ref,
    label_ref,
    noise_ref,
    logs_hbm,
    table_hbm,
    class_hbm,
    time_in_hbm,
    time_out_hbm,
    ada_hbm,
    final_ada_hbm,
    modul_ref,
    coef_ref,
    tokens_ref,
    logs,
    table,
    class_rows,
    time_in,
    time_out,
    ada,
    sems,
):
    label = label_ref[0, 0]
    block = pl.multiple_of((label // 8) * 8, 8)
    copies = [
        pltpu.make_async_copy(table_hbm, table, sems.at[0]),
        pltpu.make_async_copy(time_in_hbm, time_in, sems.at[1]),
        pltpu.make_async_copy(time_out_hbm, time_out, sems.at[2]),
        pltpu.make_async_copy(class_hbm.at[pl.ds(block, 8), :], class_rows, sems.at[3]),
        pltpu.make_async_copy(logs_hbm, logs, sems.at[4]),
    ]
    for column in range(8):
        source = ada_hbm if column < 6 else final_ada_hbm
        at = column if column < 6 else column - 6
        copies.append(
            pltpu.make_async_copy(
                source.at[:, at * D : (at + 1) * D], ada.at[column], sems.at[5 + column]
            )
        )
    for copy in copies:
        copy.start()
    tokens_ref[...] = noise_ref[...].astype(jnp.bfloat16)
    point = where_ref[3]
    now, after = timesteps_ref[point], timesteps_ref[point + 1]

    copies[0].wait()
    high = table[pl.ds(now // STEP, 1), :]
    low = table[pl.ds(STEP + now % STEP, 1), :]
    half = FREQ // 2
    high_cos, high_sin, low_cos, low_sin = high[:, :half], high[:, half:], low[:, :half], low[:, half:]
    features = jnp.concatenate(
        [high_cos * low_cos - high_sin * low_sin, high_sin * low_cos + high_cos * low_sin], axis=1
    ).astype(jnp.bfloat16)
    copies[1].wait()
    time_hidden = jax.nn.silu(matmul(features, time_in[...])).astype(jnp.bfloat16)
    copies[2].wait()
    time_embed = matmul(time_hidden, time_out[...])
    copies[3].wait()
    row = lax.broadcasted_iota(jnp.int32, (8, D), 0)
    classes = jnp.sum(
        jnp.where(row == label % 8, class_rows[...].astype(jnp.float32), 0.0), axis=0, keepdims=True
    )
    summed = jax.nn.silu(time_embed + classes).astype(jnp.bfloat16)

    copies[4].wait()
    entry = lax.broadcasted_iota(jnp.int32, (8, LANES), 0) * LANES + lax.broadcasted_iota(
        jnp.int32, (8, LANES), 1
    )

    def alpha(moment):
        found = jnp.where(entry == moment, logs[...], 0.0)
        total = jnp.sum(jnp.sum(found, axis=1, keepdims=True), axis=0, keepdims=True)
        return jnp.exp(jnp.broadcast_to(total, (8, LANES)))

    alpha_now, alpha_after = alpha(now), alpha(after)
    keep = jnp.sqrt(alpha_after / alpha_now)
    coef = jnp.sqrt(1.0 - alpha_after) - jnp.sqrt(alpha_after * (1.0 - alpha_now) / alpha_now)
    coef_ref[0:8, :] = keep - 1.0
    coef_ref[8:16, :] = coef
    for column in range(8):
        copies[5 + column].wait()
        modul_ref[:, column * D : (column + 1) * D] = matmul(summed, ada[column])


def condition(where, timesteps, labels, noise, *weights):
    return pl.pallas_call(
        condition_kernel,
        out_shape=(
            jax.ShapeDtypeStruct((1, 8 * D), jnp.float32),
            jax.ShapeDtypeStruct((16, LANES), jnp.float32),
            jax.ShapeDtypeStruct((2 * DENSE, LANES), jnp.bfloat16),
        ),
        in_specs=[SMEM] * 3 + [VMEM] + [HBM] * 7,
        out_specs=(VMEM, VMEM, VMEM),
        scratch_shapes=[
            pltpu.VMEM((8, LANES), jnp.float32),
            pltpu.VMEM((2 * STEP, FREQ), jnp.float32),
            pltpu.VMEM((8, D), jnp.bfloat16),
            pltpu.VMEM((FREQ, D), jnp.bfloat16),
            pltpu.VMEM((D, D), jnp.bfloat16),
            pltpu.VMEM((8, D, D), jnp.bfloat16),
            pltpu.SemaphoreType.DMA((13,)),
        ],
        compiler_params=pltpu.CompilerParams(vmem_limit_bytes=24 * MIB),
        name="condition",
    )(where, timesteps, labels, noise, log_table(), time_table(), *weights)


def denoise_kernel(
    where_ref,
    mixing_ref,
    tokens_ref,
    state_ref,
    modul_ref,
    coef_ref,
    coarse_hbm,
    fine_hbm,
    patch_hbm,
    kv_hbm,
    q_hbm,
    out_hbm,
    final_hbm,
    up_a_hbm,
    down_a_hbm,
    up_b_hbm,
    down_b_hbm,
    drift_ref,
    payload_ref,
    coarse_w,
    fine_w,
    patch_w,
    kv_w,
    q_w,
    out_w,
    final_w,
    up_w,
    down_w,
    hidden_all,
    queries,
    keys,
    values,
    attended,
    scores,
    sems,
):
    sources = [coarse_hbm, fine_hbm, patch_hbm, kv_hbm, q_hbm, out_hbm, final_hbm]
    sources += [up_a_hbm, down_a_hbm, up_b_hbm, down_b_hbm]
    targets = [coarse_w, fine_w, patch_w, kv_w, q_w, out_w, final_w]
    targets += [up_w.at[0], down_w.at[0], up_w.at[1], down_w.at[1]]
    copies = [
        pltpu.make_async_copy(source, target, sems.at[at])
        for at, (source, target) in enumerate(zip(sources, targets))
    ]
    for copy in copies[:5]:
        copy.start()
    member = where_ref[0]
    mods = [modul_ref[:, i * D : (i + 1) * D] for i in range(8)]
    shift_attn, scale_attn, gate_attn, shift_mlp, scale_mlp, gate_mlp, shift_out, scale_out = mods
    dense_lane = lax.broadcasted_iota(jnp.int32, (DENSE, LANES), 1) // PATCH
    for pair in range(PAIRS):
        values[pair, :, LANES:] = jnp.ones((SEQ, LANES), jnp.bfloat16)
    for copy in copies[:3]:
        copy.wait()
    patch = jnp.concatenate([patch_w[...]] * PER_ROW, axis=0)

    def embedded(dense, coarse, first_group):
        coarse_sin, coarse_cos = coarse[:, :HALF], coarse[:, HALF:]
        pieces = []
        for group in range(first_group, first_group + GROUPS):
            picked = jnp.where(dense_lane == group, dense, jnp.zeros_like(dense))
            fine_sin = fine_w[group : group + 1, 0:HALF]
            fine_cos = fine_w[group : group + 1, HALF:D]
            places = jnp.concatenate(
                [
                    coarse_sin * fine_cos + coarse_cos * fine_sin,
                    coarse_cos * fine_cos - coarse_sin * fine_sin,
                ],
                axis=1,
            )
            pieces.append(matmul(picked, patch) + places)
        return jnp.concatenate(pieces, axis=0)

    for half in range(2):
        start = pl.multiple_of((member if half == 0 else 1 - member) * DENSE, DENSE)
        dense = tokens_ref[pl.ds(start, DENSE), :]
        coarse = coarse_w[pl.ds(start, DENSE), :]
        for block in range(OWN // ROWS):
            low = block * ROWS
            hidden = embedded(dense, coarse, block * GROUPS)
            attn_in = normed(hidden, shift_attn, scale_attn).astype(jnp.bfloat16)
            if half == 0 and block == 0:
                copies[3].wait()
                copies[4].wait()
                for copy in copies[5:]:
                    copy.start()
            if half == 0:
                hidden_all[low : low + ROWS, :] = hidden
                q = (matmul(attn_in, q_w[...]) * Q_FACTOR).astype(jnp.bfloat16)
                for pair in range(PAIRS):
                    queries[pair, low : low + ROWS, :] = q[:, pair * LANES : (pair + 1) * LANES]
            both = matmul(attn_in, kv_w[...]).astype(jnp.bfloat16)
            at = half * OWN + low
            for pair in range(PAIRS):
                here = pair * LANES
                keys[pair, at : at + ROWS, :] = both[:, here : here + LANES]
                values[pair, at : at + ROWS, 0:LANES] = both[:, D + here : D + here + LANES]

    lane = lax.broadcasted_iota(jnp.int32, (ROWS, LANES), 1)

    def score(pair, block, odd, slot):
        q = queries[pair, block * ROWS : (block + 1) * ROWS, :]
        q = jnp.where((lane >= LANES // 2) == bool(odd), q, jnp.zeros_like(q))
        scores[slot] = lax.dot_general(
            q, keys[pair], (((1,), (1,)), ((), ())), preferred_element_type=jnp.float32
        )

    def weigh(pair, slot):
        s = scores[slot]
        e = jnp.exp2(s - jnp.max(s, axis=1, keepdims=True)).astype(jnp.bfloat16)
        o = matmul(e, values[pair])
        return o[:, :LANES] / o[:, LANES:]

    def over_pair(pair, carry):
        score(pair, 0, 1, 1)
        outs = [weigh(pair, 0)]
        score(pair, 1, 0, 0)
        outs.append(weigh(pair, 1))
        score(pair, 1, 1, 1)
        outs.append(weigh(pair, 0))
        score(jnp.minimum(pair + 1, PAIRS - 1), 0, 0, 0)
        outs.append(weigh(pair, 1))
        at = pl.multiple_of(pair * LANES, LANES)
        for block in range(OWN // ROWS):
            attended[block * ROWS : (block + 1) * ROWS, pl.ds(at, LANES)] = jnp.where(
                lane < LANES // 2, outs[2 * block], outs[2 * block + 1]
            ).astype(jnp.bfloat16)
        return carry

    score(0, 0, 0, 0)
    lax.fori_loop(0, PAIRS, over_pair, 0)

    eps = jnp.zeros((DENSE, LANES), jnp.float32)
    chosen = (
        lax.broadcasted_iota(jnp.int32, (PATCH, LANES), 1) % PATCH
        == lax.broadcasted_iota(jnp.int32, (PATCH, LANES), 0)
    ).astype(jnp.bfloat16)
    copies[5].wait()
    copies[6].wait()
    final_tiled = matmul(final_w[...], chosen).astype(jnp.bfloat16)
    for block in range(OWN // ROWS):
        rows = slice(block * ROWS, (block + 1) * ROWS)
        h1 = hidden_all[rows, :] + gate_attn * matmul(attended[rows, :], out_w[...])
        mlp_in = normed(h1, shift_mlp, scale_mlp).astype(jnp.bfloat16)
        mlp_out = None
        for part in range(2):
            if block == 0:
                copies[7 + 2 * part].wait()
            lifted = jax.nn.gelu(matmul(mlp_in, up_w[part]), approximate=True).astype(jnp.bfloat16)
            if block == 0:
                copies[8 + 2 * part].wait()
            share = matmul(lifted, down_w[part]).astype(jnp.bfloat16).astype(jnp.float32)
            mlp_out = share if part == 0 else mlp_out + share
        h2 = h1 + gate_mlp * mlp_out
        final_in = normed(h2, shift_out, scale_out).astype(jnp.bfloat16)
        predicted = matmul(final_in, final_tiled)
        for group in range(GROUPS):
            eps = jnp.where(
                dense_lane == block * GROUPS + group,
                predicted[group * DENSE : (group + 1) * DENSE, :],
                eps,
            )
    drift = coef_ref[0:1, :] * state_ref[...] + coef_ref[8:9, :] * eps
    drift_ref[...] = drift
    mixing = jnp.full((EXTRA, LANES), mixing_ref[0, 0], jnp.float32)
    rounded = mixing.astype(jnp.bfloat16).astype(jnp.float32)
    row = lax.broadcasted_iota(jnp.int32, (EXTRA, LANES), 0)
    beside = jnp.where(row == 0, rounded, jnp.where(row == 1, mixing - rounded, 0.0))
    sent = jnp.concatenate([drift, beside], axis=0).astype(jnp.bfloat16)
    for copy in range(payload_ref.shape[0]):
        payload_ref[copy] = sent


def denoise(copies, where, mixing, tokens, state, modul, coefs, *weights):
    bf16 = jnp.bfloat16
    return pl.pallas_call(
        denoise_kernel,
        out_shape=(
            jax.ShapeDtypeStruct((DENSE, LANES), jnp.float32),
            jax.ShapeDtypeStruct((copies, FULL, LANES), bf16),
        ),
        in_specs=[SMEM] * 2 + [VMEM] * 4 + [HBM] * 11,
        out_specs=(VMEM, VMEM),
        scratch_shapes=[
            pltpu.VMEM((SEQ // PER_ROW, D), jnp.float32),
            pltpu.VMEM((PER_ROW, D), jnp.float32),
            pltpu.VMEM((PATCH, D), bf16),
            pltpu.VMEM((D, 2 * D), bf16),
            pltpu.VMEM((D, D), bf16),
            pltpu.VMEM((D, D), bf16),
            pltpu.VMEM((D, PATCH), bf16),
            pltpu.VMEM((2, D, FF_OWN), bf16),
            pltpu.VMEM((2, FF_OWN, D), bf16),
            pltpu.VMEM((OWN, D), jnp.float32),
            pltpu.VMEM((PAIRS, OWN, LANES), bf16),
            pltpu.VMEM((PAIRS, SEQ, LANES), bf16),
            pltpu.VMEM((PAIRS, SEQ, 2 * LANES), bf16),
            pltpu.VMEM((OWN, D), bf16),
            pltpu.VMEM((2, ROWS, SEQ), jnp.float32),
            pltpu.SemaphoreType.DMA((11,)),
        ],
        compiler_params=pltpu.CompilerParams(vmem_limit_bytes=48 * MIB),
        name="denoise",
    )(where, mixing, tokens, state, modul, coefs, *weights)


def plane_kernel(where_ref, pieces_ref, inside_ref, payload_ref):
    here = where_ref[1]
    count = pieces_ref.shape[0]
    before = jnp.zeros((DENSE, LANES), jnp.float32)
    total = before
    beside = jnp.zeros((EXTRA, LANES), jnp.float32)
    for k in range(count):
        piece = pieces_ref[k].astype(jnp.float32)
        before = before + jnp.where(k < here, piece[:DENSE], 0.0)
        total = total + piece[:DENSE]
        beside = jnp.where(k == here - 1, piece[DENSE:], beside)
    inside_ref[0:DENSE, :] = before
    inside_ref[DENSE:FULL, :] = beside
    last = pieces_ref[count - 1, DENSE:FULL, :].astype(jnp.float32)
    sent = jnp.concatenate([total, last], axis=0).astype(jnp.bfloat16)
    for copy in range(payload_ref.shape[0]):
        payload_ref[copy] = sent


def plane(where, pieces, planes):
    return pl.pallas_call(
        plane_kernel,
        out_shape=(
            jax.ShapeDtypeStruct((FULL, LANES), jnp.float32),
            jax.ShapeDtypeStruct((planes, FULL, LANES), jnp.bfloat16),
        ),
        in_specs=[SMEM, VMEM],
        out_specs=(VMEM, VMEM),
        compiler_params=pltpu.CompilerParams(vmem_limit_bytes=8 * MIB),
        name="plane",
    )(where, pieces)


def entered(where_ref, planes_ref, inside_ref):
    before = inside_ref[0:DENSE, :]
    for k in range(planes_ref.shape[0]):
        piece = planes_ref[k, 0:DENSE, :].astype(jnp.float32)
        before = before + jnp.where(k < where_ref[2], piece, 0.0)
    return before


def advance_kernel(
    where_ref, planes_ref, inside_ref, drift_ref, noise_ref, reached_ref, state_ref, tokens_ref
):
    before = entered(where_ref, planes_ref, inside_ref)
    reached_ref[...] = before + drift_ref[...]
    beside = inside_ref[DENSE:FULL, :]
    for k in range(planes_ref.shape[0]):
        found = jnp.logical_and(where_ref[1] == 0, k == where_ref[2] - 1)
        beside = jnp.where(found, planes_ref[k, DENSE:FULL, :].astype(jnp.float32), beside)
    mixing = jnp.sum(beside, axis=0, keepdims=True)
    start = pl.multiple_of(where_ref[0] * DENSE, DENSE)
    state = noise_ref[pl.ds(start, DENSE), :] + (1.0 + mixing) * before
    state_ref[...] = state
    tokens_ref[...] = state.astype(jnp.bfloat16)


def advance(where, planes, inside, drift, noise):
    field = jax.ShapeDtypeStruct((DENSE, LANES), jnp.float32)
    return pl.pallas_call(
        advance_kernel,
        out_shape=(field, field, jax.ShapeDtypeStruct((DENSE, LANES), jnp.bfloat16)),
        in_specs=[SMEM] + [VMEM] * 4,
        out_specs=(VMEM, VMEM, VMEM),
        compiler_params=pltpu.CompilerParams(vmem_limit_bytes=8 * MIB),
        name="advance",
    )(where, planes, inside, drift, noise)


def close_kernel(
    where_ref, mixing_ref, planes_ref, inside_ref, drift_ref, noise_ref, first_ref, packed_ref
):
    reached = entered(where_ref, planes_ref, inside_ref) + drift_ref[...]
    first = first_ref[...]
    start = pl.multiple_of(where_ref[0] * DENSE, DENSE)
    packed_ref[0:DENSE, :] = (
        noise_ref[pl.ds(start, DENSE), :] + reached + mixing_ref[1, 0] * (reached - first)
    )
    missed = reached - (1.0 + mixing_ref[0, 0]) * first

    def total(values):
        return jnp.sum(jnp.sum(values * values, axis=1, keepdims=True), axis=0, keepdims=True)

    row = lax.broadcasted_iota(jnp.int32, (EXTRA, LANES), 0)
    packed_ref[DENSE:FULL, :] = jnp.where(row == 0, total(first), total(missed)) / (
        2 * DENSE * LANES
    )


def close(where, mixing, planes, inside, drift, noise, first):
    return pl.pallas_call(
        close_kernel,
        out_shape=jax.ShapeDtypeStruct((FULL, LANES), jnp.float32),
        in_specs=[SMEM] * 2 + [VMEM] * 5,
        out_specs=VMEM,
        compiler_params=pltpu.CompilerParams(vmem_limit_bytes=8 * MIB),
        name="close",
    )(where, mixing, planes, inside, drift, noise, first)


def exchanged(copies, axis):
    return lax.all_to_all(copies, axis, split_axis=0, concat_axis=0, tiled=True)


def per_device(
    noise_start,
    timesteps,
    class_labels,
    mixing,
    class_table,
    time_in,
    time_out,
    ada_weight,
    final_ada,
    patch_weight,
    q_weight,
    kv_weight,
    out_weight,
    up_weight,
    down_weight,
    final_weight,
):
    swap = [(0, 1), (1, 0)]
    up_other = lax.ppermute(up_weight, "tensor", swap)
    down_other = lax.ppermute(down_weight, "tensor", swap)
    where = jnp.stack(
        [lax.axis_index(axis) for axis in ("tensor", PLANE, "tm_0", TM)]
    ).astype(jnp.int32)
    noise = noise_start.reshape(2 * DENSE, LANES)
    modul, coefs, tokens = condition(
        where,
        timesteps,
        class_labels,
        noise,
        class_table,
        time_in,
        time_out,
        ada_weight,
        final_ada,
    )
    coarse, fine = place_tables()
    weights = (coarse, fine, patch_weight, kv_weight, q_weight, out_weight, final_weight)
    weights += (up_weight, down_weight, up_other, down_other)

    def scanned(tokens, state):
        drift, payload = denoise(
            lax.axis_size(PLANE), where, mixing, tokens, state, modul, coefs, *weights
        )
        pieces = exchanged(payload, PLANE)
        inside, payload = plane(where, pieces, lax.axis_size("tm_0"))
        return drift, inside, exchanged(payload, "tm_0")

    noise_own = lax.dynamic_slice_in_dim(noise, where[0] * DENSE, DENSE, 0)
    drift, inside, planes = scanned(tokens, noise_own)
    reached, state, tokens = advance(where, planes, inside, drift, noise)
    tokens = lax.all_gather(tokens, "tensor", tiled=True)
    drift, inside, planes = scanned(tokens, state)
    packed = lax.all_gather(
        close(where, mixing, planes, inside, drift, noise, reached), "tensor"
    )
    states = packed[:, :DENSE].reshape(1, 1, 2 * DENSE * LANES)
    residuals = packed[0, DENSE : DENSE + ITERS, :1] + packed[1, DENSE : DENSE + ITERS, :1]
    return (states, residuals)


def solution(mesh):
    split = Mesh(
        mesh.devices.reshape(8, 4, 4, mesh.shape["tensor"]), ("tm_0", "tm_1", "tm_2", "tensor")
    )
    placed = (
        P(),
        P(),
        P(TM, None),
        P(None, TM),
        P(),
        P(),
        P(),
        P(),
        P(),
        P(),
        P(),
        P(),
        P(),
        P(None, "tensor"),
        P("tensor", None),
        P(),
    )
    return jax.shard_map(
        per_device,
        mesh=split,
        in_specs=placed,
        out_specs=(P(TM, None, None), P(None, TM)),
        check_vma=False,
    )
```

profile of v0, /device:TPU:1, one launch (start us, length us, event | category | flops | bytes accessed | tf_op | source)
XLA Modules:
  0.0 138.1 jit_solution(14086905695997580810)
XLA Ops:
  0.6 3.3 %collective-permute-start = (bf16[768,1536]{1,0:T(8,128)(2,1)}, bf16[768,1536]{1,0:T(8,128)(2,1)S(1)}, u32[]{:S(2)}, u32[]{:S(2)}) collective-permute-start(bf16[768,1536]{1,0:T(8,128)(2,1)} %up_a_hbm.3), channel_id=1, source_target_pairs={{0,1},{1,0},{2,3},{3,2},{4,5},{5,4},{6,7},{7,6},{8,9},{9,8},{10,11... | collective-permute-start | bytes 7077896 | tf_op jit(solution)/shard_map/ppermute | solution.py:523
  4.7 0.7 copy.26.mixing_ref
  5.4 0.9 copy.23.final_hbm
  6.4 3.0 %copy-done.1 = bf16[768,4608]{1,0:T(8,128)(2,1)S(1)} copy-done((bf16[768,4608]{1,0:T(8,128)(2,1)S(1)}, bf16[768,4608]{1,0:T(8,128)(2,1)}, u32[]{:S(2)}) %copy-start.1) | copy-done | bytes 7077912
  9.4 1.7 %copy-done.4 = bf16[768,1536]{1,0:T(8,128)(2,1)S(1)} copy-done((bf16[768,1536]{1,0:T(8,128)(2,1)S(1)}, bf16[768,1536]{1,0:T(8,128)(2,1)}, u32[]{:S(2)}) %copy-start.4) | copy-done | bytes 2359320
  11.1 1.4 %copy-done.6 = bf16[1000,768]{1,0:T(8,128)(2,1)S(1)} copy-done((bf16[1000,768]{1,0:T(8,128)(2,1)S(1)}, bf16[1000,768]{1,0:T(8,128)(2,1)}, u32[]{:S(2)}) %copy-start.6) | copy-done | bytes 1536024
  12.5 1.3 copy-done.7
  13.8 0.8 copy-done.8
  14.6 1.0 copy-done.10
  15.6 0.8 copy-done.13
  16.4 0.7 copy-done.14
  17.1 0.7 copy-done.15
  17.8 5.2 %condition.1 = (f32[1,6144]{1,0:T(1,128)S(1)}, f32[16,128]{1,0:T(8,128)S(1)}, bf16[128,128]{1,0:T(8,128)(2,1)S(1)}) custom-call(s32[4]{0:T(128)S(1)} %pad_add_fusion.where_ref, s32[129]{0:T(256)S(1)} %copy-done.15, s32[1,1]{1,0:T(1,128)S(6)} %copy.31.label_ref, f32[128,128]{1,0:T(8,128)S(1)} %bitcast.9, f32[8,128]{1,0:T(8,128)S(1)} %copy-done.14, ...), custom_call_target="tpu_custom_call" | custom-call | tf_op jit(solution)/shard_map/condition/pallas_call | solution.py:170
  23.1 1.4 %copy-done.16 = bf16[768,1536]{1,0:T(8,128)(2,1)} copy-done((bf16[768,1536]{1,0:T(8,128)(2,1)}, bf16[768,1536]{1,0:T(8,128)(2,1)S(1)}, u32[]{:S(2)}) %copy-start.16) | copy-done | bytes 2359320
  24.5 24.9 %denoise.2 = (f32[64,128]{1,0:T(8,128)S(1)}, bf16[16,72,128]{2,1,0:T(8,128)(2,1)S(1)}) custom-call(s32[4]{0:T(128)S(1)} %pad_add_fusion.where_ref, f32[2,1]{1,0:T(2,128)S(1)} %copy.26.mixing_ref, bf16[128,128]{1,0:T(8,128)(2,1)S(1)} %get-tuple-element.16.tokens_ref, f32[64,128]{1,0:T(8,128)S(1)} %constant_dynamic-slice_fusion.state_ref, ...), custom_call_target="tpu_custom_call" | custom-call | tf_op jit(solution)/shard_map/denoise/pallas_call | solution.py:369
  49.4 13.3 %all_to_all.20.pieces_ref = bf16[16,72,128]{2,1,0:T(8,128)(2,1)S(1)} all-to-all(bf16[16,72,128]{2,1,0:T(8,128)(2,1)S(1)} %get-tuple-element.19), channel_id=1, replica_groups=mesh['tm_0'=8,'tm_1'=4,'tm_2'=4,'tensor'=2] {'tm_1','tm_2'}, dimensions={0} | all-to-all | bytes 589824 | tf_op jit(solution)/shard_map/all_to_all | solution.py:501
  63.4 16.1 %all_to_all.21.planes_ref = bf16[8,72,128]{2,1,0:T(8,128)(2,1)S(1)} all-to-all(bf16[8,72,128]{2,1,0:T(8,128)(2,1)S(1)} %get-tuple-element.20), channel_id=1, replica_groups=mesh['tm_0'=8,'tm_1'=4,'tm_2'=4,'tensor'=2] {'tm_0'}, dimensions={0} | all-to-all | bytes 294912 | tf_op jit(solution)/shard_map/all_to_all | solution.py:501
  80.1 4.4 %all_gather.9.tokens_ref = bf16[128,128]{1,0:T(8,128)(2,1)S(1)} all-gather(bf16[64,128]{1,0:T(8,128)(2,1)S(1)} %get-tuple-element.23), channel_id=1, replica_groups=mesh['tm_0'=8,'tm_1'=4,'tm_2'=4,'tensor'=2] {'tensor'}, dimensions={0}, use_global_device_ids=true | all-gather | bytes 49152 | tf_op jit(solution)/shard_map/all_gather | solution.py:555
  84.5 25.2 %denoise.3 = (f32[64,128]{1,0:T(8,128)S(1)}, bf16[16,72,128]{2,1,0:T(8,128)(2,1)S(1)}) custom-call(s32[4]{0:T(128)S(1)} %pad_add_fusion.where_ref, f32[2,1]{1,0:T(2,128)S(1)} %copy.26.mixing_ref, bf16[128,128]{1,0:T(8,128)(2,1)S(1)} %all_gather.9.tokens_ref, f32[64,128]{1,0:T(8,128)S(1)} %get-tuple-element.24.state_ref, ...), custom_call_target="tpu_custom_call" | custom-call | tf_op jit(solution)/shard_map/denoise/pallas_call | solution.py:369
  109.7 11.1 %all_to_all.22.pieces_ref = bf16[16,72,128]{2,1,0:T(8,128)(2,1)S(1)} all-to-all(bf16[16,72,128]{2,1,0:T(8,128)(2,1)S(1)} %get-tuple-element.25), channel_id=1, replica_groups=mesh['tm_0'=8,'tm_1'=4,'tm_2'=4,'tensor'=2] {'tm_1','tm_2'}, dimensions={0} | all-to-all | bytes 589824 | tf_op jit(solution)/shard_map/all_to_all | solution.py:501
  121.5 10.6 %all_to_all.23.planes_ref = bf16[8,72,128]{2,1,0:T(8,128)(2,1)S(1)} all-to-all(bf16[8,72,128]{2,1,0:T(8,128)(2,1)S(1)} %get-tuple-element.26), channel_id=1, replica_groups=mesh['tm_0'=8,'tm_1'=4,'tm_2'=4,'tensor'=2] {'tm_0'}, dimensions={0} | all-to-all | bytes 294912 | tf_op jit(solution)/shard_map/all_to_all | solution.py:501
  132.1 0.7 close.1
  132.7 4.0 %all-gather = f32[144,128]{1,0:T(8,128)S(1)} all-gather(f32[72,128]{1,0:T(8,128)S(1)} %close.1), channel_id=2, replica_groups=mesh['tm_0'=8,'tm_1'=4,'tm_2'=4,'tensor'=2] {'tensor'}, dimensions={0}, use_global_device_ids=true | all-gather | bytes 110592 | tf_op jit(solution)/shard_map/all_gather | solution.py:557
  136.8 0.6 slice.12
  (36 shorter events, 2.8 us)
Async XLA Ops:
  0.6 22.4 %collective-permute-start = (bf16[768,1536]{1,0:T(8,128)(2,1)}, bf16[768,1536]{1,0:T(8,128)(2,1)S(1)}, u32[]{:S(2)}, u32[]{:S(2)}) collective-permute-start(bf16[768,1536]{1,0:T(8,128)(2,1)} %up_a_hbm.3), channel_id=1, source_target_pairs={{0,1},{1,0},{2,3},{3,2},{4,5},{5,4},{6,7},{7,6},{8,9},{9,8},{10,11... | collective-permute-start | bytes 7077896 | tf_op jit(solution)/shard_map/ppermute | solution.py:523
  3.9 19.1 %collective-permute-start.1 = (bf16[1536,768]{1,0:T(8,128)(2,1)}, bf16[1536,768]{1,0:T(8,128)(2,1)}, u32[]{:S(2)}, u32[]{:S(2)}) collective-permute-start(bf16[1536,768]{1,0:T(8,128)(2,1)} %down_a_hbm.3), channel_id=1, source_target_pairs={{0,1},{1,0},{2,3},{3,2},{4,5},{5,4},{6,7},{7,6},{8,9},{9,8},{10,11... | collective-permute-start | bytes 7077896 | tf_op jit(solution)/shard_map/ppermute | solution.py:524
  6.4 3.0 %copy-start.1 = (bf16[768,4608]{1,0:T(8,128)(2,1)S(1)}, bf16[768,4608]{1,0:T(8,128)(2,1)}, u32[]{:S(2)}) copy-start(bf16[768,4608]{1,0:T(8,128)(2,1)} %ada_hbm.1) | copy-start | bytes 21233668
  9.4 1.7 %copy-start.4 = (bf16[768,1536]{1,0:T(8,128)(2,1)S(1)}, bf16[768,1536]{1,0:T(8,128)(2,1)}, u32[]{:S(2)}) copy-start(bf16[768,1536]{1,0:T(8,128)(2,1)} %final_ada_hbm.1) | copy-start | bytes 7077892
  11.1 1.4 %copy-start.6 = (bf16[1000,768]{1,0:T(8,128)(2,1)S(1)}, bf16[1000,768]{1,0:T(8,128)(2,1)}, u32[]{:S(2)}) copy-start(bf16[1000,768]{1,0:T(8,128)(2,1)} %class_hbm.1) | copy-start | bytes 4608004
  12.5 1.3 copy-start.7
  13.8 0.8 copy-start.8
  14.6 1.0 copy-start.10
  15.6 0.8 copy-start.13
  16.4 0.7 copy-start.14
  17.1 0.7 copy-start.15
  17.8 6.7 %copy-start = (bf16[768,1536]{1,0:T(8,128)(2,1)S(1)}, bf16[768,1536]{1,0:T(8,128)(2,1)}, u32[]{:S(2)}) copy-start(bf16[768,1536]{1,0:T(8,128)(2,1)} %kv_hbm.3) | copy-start | bytes 7077892
  17.8 6.7 %copy-start.2 = (bf16[768,768]{1,0:T(8,128)(2,1)S(1)}, bf16[768,768]{1,0:T(8,128)(2,1)}, u32[]{:S(2)}) copy-start(bf16[768,768]{1,0:T(8,128)(2,1)} %q_hbm.3) | copy-start | bytes 3538948
  17.8 6.7 %copy-start.3 = (bf16[768,768]{1,0:T(8,128)(2,1)S(1)}, bf16[768,768]{1,0:T(8,128)(2,1)}, u32[]{:S(2)}) copy-start(bf16[768,768]{1,0:T(8,128)(2,1)} %out_hbm.3) | copy-start | bytes 3538948
  17.8 6.7 %copy-start.5 = (f32[128,768]{1,0:T(8,128)S(1)}, f32[128,768]{1,0:T(8,128)}, u32[]{:S(2)}) copy-start(f32[128,768]{1,0:T(8,128)} %constant.36.clone.coarse_hbm) | copy-start | bytes 1179652
  17.8 6.7 %copy-start.11 = (bf16[16,768]{1,0:T(8,128)(2,1)S(1)}, bf16[16,768]{1,0:T(8,128)(2,1)}, u32[]{:S(2)}) copy-start(bf16[16,768]{1,0:T(8,128)(2,1)} %patch_hbm.3) | copy-start | bytes 73732
  17.8 6.7 %copy-start.12 = (f32[8,768]{1,0:T(8,128)S(1)}, f32[8,768]{1,0:T(8,128)}, u32[]{:S(2)}) copy-start(f32[8,768]{1,0:T(8,128)} %constant.37.clone.fine_hbm) | copy-start | bytes 73732
  23.0 1.4 %copy-start.16 = (bf16[768,1536]{1,0:T(8,128)(2,1)}, bf16[768,1536]{1,0:T(8,128)(2,1)S(1)}, u32[]{:S(2)}) copy-start(bf16[768,1536]{1,0:T(8,128)(2,1)S(1)} %collective-permute-done.up_b_hbm) | copy-start | bytes 7077892
  24.5 55.0 %copy-start.9 = (f32[1,16384]{1,0:T(1,128)S(1)}, f32[1,16384]{1,0:T(1,128)}, u32[]{:S(2)}) copy-start(f32[1,16384]{1,0:T(1,128)} %param.20) | copy-start | bytes 196612
where the time goes:
time: 139 us; the launch traced here: 138 us
  blocking collectives  59.6 us (43%)
  Pallas kernels  57.8 us (42%)
  local copies, waits for them, and re-layouts  15.3 us (11%)
  starting transfers between devices  3.39 us (2%)
  between operations  1.44 us (1%)
    all_to_all x4, blocking collectives, exchanged(): return lax.all_to_all(copies, axis, split_axis=0, concat_axis=0, tiled=True)  51.1 us
    pallas_call x2, Pallas kernels, denoise(): pl.pallas_call(denoise_kernel, out_shape=(jax.ShapeDtypeStruct((DENSE, LA...  50.1 us
    unnamed x38, local copies, waits for them, and re-layouts  14.7 us
    pallas_call x1, Pallas kernels, condition(): pl.pallas_call(condition_kernel, out_shape=(jax.ShapeDtypeStruct((1, 8 *...  5.17 us
    all_gather x1, blocking collectives, per_device(): tokens = lax.all_gather(tokens, 'tensor', tiled=True)  4.45 us
    all_gather x1, blocking collectives, per_device(): lax.all_gather(close(where, mixing, planes, inside, drift, noise, reached...  4.05 us
    ppermute x1, starting transfers between devices, per_device(): up_other = lax.ppermute(up_weight, 'tensor', swap)  3.29 us
  transfers between devices with their start and end apart: 2, of which 0 were waited for; matrix products, arithmetic and copies ran while one was open for 1% of the time, Pallas kernels for 4%

commit v1 on v0

--- a/solution.py
+++ b/solution.py
@@ -29,6 +29,8 @@
 HALF = D // 2
 ROWS = 256
 GROUPS = ROWS // DENSE
+MLP_ROWS = 512
+MLP_CHUNK = 768
 MIB = 1 << 20
 EXTRA = 8
 FULL = DENSE + EXTRA
@@ -185,7 +187,7 @@
             pltpu.VMEM((8, D, D), jnp.bfloat16),
             pltpu.SemaphoreType.DMA((13,)),
         ],
-        compiler_params=pltpu.CompilerParams(vmem_limit_bytes=24 * MIB),
+        compiler_params=pltpu.CompilerParams(vmem_limit_bytes=62 * MIB),
         name="condition",
     )(where, timesteps, labels, noise, log_table(), time_table(), *weights)
 
@@ -331,25 +333,34 @@
     copies[5].wait()
     copies[6].wait()
     final_tiled = matmul(final_w[...], chosen).astype(jnp.bfloat16)
-    for block in range(OWN // ROWS):
-        rows = slice(block * ROWS, (block + 1) * ROWS)
+    for copy in copies[7:]:
+        copy.wait()
+    for block in range(OWN // MLP_ROWS):
+        rows = slice(block * MLP_ROWS, (block + 1) * MLP_ROWS)
         h1 = hidden_all[rows, :] + gate_attn * matmul(attended[rows, :], out_w[...])
         mlp_in = normed(h1, shift_mlp, scale_mlp).astype(jnp.bfloat16)
         mlp_out = None
-        for part in range(2):
-            if block == 0:
-                copies[7 + 2 * part].wait()
-            lifted = jax.nn.gelu(matmul(mlp_in, up_w[part]), approximate=True).astype(jnp.bfloat16)
-            if block == 0:
-                copies[8 + 2 * part].wait()
-            share = matmul(lifted, down_w[part]).astype(jnp.bfloat16).astype(jnp.float32)
-            mlp_out = share if part == 0 else mlp_out + share
+        steps = [(part, at) for part in range(2) for at in range(0, FF_OWN, MLP_CHUNK)]
+
+        def raised(step):
+            return matmul(mlp_in, up_w[step[0], :, step[1] : step[1] + MLP_CHUNK])
+
+        ahead = raised(steps[0])
+        shares = [None, None]
+        for index, (part, at) in enumerate(steps):
+            now = ahead
+            if index + 1 < len(steps):
+                ahead = raised(steps[index + 1])
+            lifted = jax.nn.gelu(now, approximate=True).astype(jnp.bfloat16)
+            product = matmul(lifted, down_w[part, at : at + MLP_CHUNK, :])
+            shares[part] = product if shares[part] is None else shares[part] + product
+        mlp_out = sum(share.astype(jnp.bfloat16).astype(jnp.float32) for share in shares)
         h2 = h1 + gate_mlp * mlp_out
         final_in = normed(h2, shift_out, scale_out).astype(jnp.bfloat16)
         predicted = matmul(final_in, final_tiled)
-        for group in range(GROUPS):
+        for group in range(MLP_ROWS // DENSE):
             eps = jnp.where(
-                dense_lane == block * GROUPS + group,
+                dense_lane == block * (MLP_ROWS // DENSE) + group,
                 predicted[group * DENSE : (group + 1) * DENSE, :],
                 eps,
             )
@@ -392,7 +403,7 @@
             pltpu.VMEM((2, ROWS, SEQ), jnp.float32),
             pltpu.SemaphoreType.DMA((11,)),
         ],
-        compiler_params=pltpu.CompilerParams(vmem_limit_bytes=48 * MIB),
+        compiler_params=pltpu.CompilerParams(vmem_limit_bytes=61 * MIB),
         name="denoise",
     )(where, mixing, tokens, state, modul, coefs, *weights)
 

time: 139 us -> 132 us (0.950)
  local copies, waits for them, and re-layouts: 15.3 us -> 6.45 us
  blocking collectives: 59.6 us -> 61 us
    unnamed x38 -> x18, local copies, waits for them, and re-layouts: 14.7 us -> 5.2 us
  transfers between devices with their start and end apart: 2 -> 2, of which waited for: 0 -> 0; matrix products, arithmetic and copies ran while one was open for 1% -> 3% of each run, Pallas kernels for 4% -> 5%
where the time goes in v1:
time: 132 us; the launch traced here: 131 us
  blocking collectives  61 us (46%)
  Pallas kernels  57.9 us (44%)
  local copies, waits for them, and re-layouts  6.45 us (5%)
  starting transfers between devices  3.39 us (3%)
  between operations  1.36 us (1%)
    all_to_all x4, blocking collectives, exchanged(): return lax.all_to_all(copies, axis, split_axis=0, concat_axis=0, tiled=True)  52.1 us
    pallas_call x2, Pallas kernels, denoise(): pl.pallas_call(denoise_kernel, out_shape=(jax.ShapeDtypeStruct((DENSE, LA...  49.2 us
    pallas_call x1, Pallas kernels, condition(): pl.pallas_call(condition_kernel, out_shape=(jax.ShapeDtypeStruct((1, 8 *...  6.22 us
    unnamed x18, local copies, waits for them, and re-layouts  5.2 us
    all_gather x1, blocking collectives, per_device(): tokens = lax.all_gather(tokens, 'tensor', tiled=True)  4.79 us
    all_gather x1, blocking collectives, per_device(): lax.all_gather(close(where, mixing, planes, inside, drift, noise, reached...  4.09 us
    ppermute x1, starting transfers between devices, per_device(): up_other = lax.ppermute(up_weight, 'tensor', swap)  3.29 us
  transfers between devices with their start and end apart: 2, of which 0 were waited for; matrix products, arithmetic and copies ran while one was open for 3% of the time, Pallas kernels for 5%

profile of v1, /device:TPU:1, one launch (start us, length us, event | category | flops | bytes accessed | tf_op | source)
XLA Modules:
  0.0 131.3 jit_solution(973310900707741626)
XLA Ops:
  0.6 3.3 %collective-permute-start = (bf16[768,1536]{1,0:T(8,128)(2,1)}, bf16[768,1536]{1,0:T(8,128)(2,1)}, u32[]{:S(2)}, u32[]{:S(2)}) collective-permute-start(bf16[768,1536]{1,0:T(8,128)(2,1)} %up_a_hbm.3), channel_id=1, source_target_pairs={{0,1},{1,0},{2,3},{3,2},{4,5},{5,4},{6,7},{7,6},{8,9},{9,8},{10,11... | collective-permute-start | bytes 7077896 | tf_op jit(solution)/shard_map/ppermute | solution.py:534
  3.9 0.1 collective-permute-start.1
  4.7 1.3 %copy.26.mixing_ref = f32[2,1]{1,0:T(2,128)} copy(f32[2,1]{0,1:T(1,128)} %param.23) | data formatting | bytes 16 | tf_op args[3]
  6.0 1.5 %copy.23.final_hbm = bf16[768,16]{1,0:T(8,128)(2,1)} copy(bf16[768,16]{0,1:T(8,128)(2,1)} %param.35) | data formatting | bytes 49152 | tf_op args[15]
  7.5 0.6 pad_add_fusion.where_ref
  8.2 6.2 %condition.1 = (f32[1,6144]{1,0:T(1,128)}, f32[16,128]{1,0:T(8,128)}, bf16[128,128]{1,0:T(8,128)(2,1)}) custom-call(s32[4]{0:T(128)} %pad_add_fusion.where_ref, s32[129]{0:T(256)} %timesteps_ref.1, s32[1,1]{1,0:T(1,128)S(6)} %copy.31.label_ref, f32[128,128]{1,0:T(8,128)} %bitcast.9, f32[8,128]{1,0:T(8,128)} %constant.34.clone.logs_hbm, ...), custom_call_target="tpu_custom_call" | custom-call | tf_op jit(solution)/shard_map/condition/pallas_call | solution.py:172
  14.4 0.6 constant_dynamic-slice_fusion.state_ref
  15.1 24.7 %denoise.2 = (f32[64,128]{1,0:T(8,128)}, bf16[16,72,128]{2,1,0:T(8,128)(2,1)}) custom-call(s32[4]{0:T(128)} %pad_add_fusion.where_ref, f32[2,1]{1,0:T(2,128)} %copy.26.mixing_ref, bf16[128,128]{1,0:T(8,128)(2,1)} %get-tuple-element.16.tokens_ref, f32[64,128]{1,0:T(8,128)} %constant_dynamic-slice_fusion.state_ref, f32[1,6144]{1,0:T(1,128)} %get-tuple-element.17.modul_ref, ...), custom_call_target="tpu_custom_call" | custom-call | tf_op jit(solution)/shard_map/denoise/pallas_call | solution.py:380
  39.7 13.5 %all_to_all.20.pieces_ref = bf16[16,72,128]{2,1,0:T(8,128)(2,1)S(1)} all-to-all(bf16[16,72,128]{2,1,0:T(8,128)(2,1)} %get-tuple-element.19), channel_id=1, replica_groups=mesh['tm_0'=8,'tm_1'=4,'tm_2'=4,'tensor'=2] {'tm_1','tm_2'}, dimensions={0} | all-to-all | bytes 589824 | tf_op jit(solution)/shard_map/all_to_all | solution.py:512
  53.2 0.6 plane.2
  53.9 16.1 %all_to_all.21.planes_ref = bf16[8,72,128]{2,1,0:T(8,128)(2,1)S(1)} all-to-all(bf16[8,72,128]{2,1,0:T(8,128)(2,1)S(1)} %get-tuple-element.20), channel_id=1, replica_groups=mesh['tm_0'=8,'tm_1'=4,'tm_2'=4,'tensor'=2] {'tm_0'}, dimensions={0} | all-to-all | bytes 294912 | tf_op jit(solution)/shard_map/all_to_all | solution.py:512
  70.0 0.8 copy-done.2
  70.7 0.6 advance.1
  71.3 0.6 copy-done.1
  71.9 4.8 %all_gather.9.tokens_ref = bf16[128,128]{1,0:T(8,128)(2,1)} all-gather(bf16[64,128]{1,0:T(8,128)(2,1)S(1)} %get-tuple-element.23), channel_id=1, replica_groups=mesh['tm_0'=8,'tm_1'=4,'tm_2'=4,'tensor'=2] {'tensor'}, dimensions={0}, use_global_device_ids=true | all-gather | bytes 49152 | tf_op jit(solution)/shard_map/all_gather | solution.py:566
  76.7 24.5 %denoise.3 = (f32[64,128]{1,0:T(8,128)}, bf16[16,72,128]{2,1,0:T(8,128)(2,1)}) custom-call(s32[4]{0:T(128)} %pad_add_fusion.where_ref, f32[2,1]{1,0:T(2,128)} %copy.26.mixing_ref, bf16[128,128]{1,0:T(8,128)(2,1)} %all_gather.9.tokens_ref, f32[64,128]{1,0:T(8,128)} %copy-done.1, f32[1,6144]{1,0:T(1,128)} %get-tuple-element.17.modul_ref, ...), custom_call_target="tpu_custom_call" | custom-call | tf_op jit(solution)/shard_map/denoise/pallas_call | solution.py:380
  101.2 12.3 %all_to_all.22.pieces_ref = bf16[16,72,128]{2,1,0:T(8,128)(2,1)S(1)} all-to-all(bf16[16,72,128]{2,1,0:T(8,128)(2,1)} %get-tuple-element.25), channel_id=1, replica_groups=mesh['tm_0'=8,'tm_1'=4,'tm_2'=4,'tensor'=2] {'tm_1','tm_2'}, dimensions={0} | all-to-all | bytes 589824 | tf_op jit(solution)/shard_map/all_to_all | solution.py:512
  113.5 0.6 plane.3
  114.1 10.3 %all_to_all.23.planes_ref = bf16[8,72,128]{2,1,0:T(8,128)(2,1)S(1)} all-to-all(bf16[8,72,128]{2,1,0:T(8,128)(2,1)S(1)} %get-tuple-element.26), channel_id=1, replica_groups=mesh['tm_0'=8,'tm_1'=4,'tm_2'=4,'tensor'=2] {'tm_0'}, dimensions={0} | all-to-all | bytes 294912 | tf_op jit(solution)/shard_map/all_to_all | solution.py:512
  124.4 0.8 copy-done.3
  125.2 0.7 close.1
  125.9 4.1 %all-gather = f32[144,128]{1,0:T(8,128)S(1)} all-gather(f32[72,128]{1,0:T(8,128)S(1)} %close.1), channel_id=2, replica_groups=mesh['tm_0'=8,'tm_1'=4,'tm_2'=4,'tensor'=2] {'tensor'}, dimensions={0}, use_global_device_ids=true | all-gather | bytes 110592 | tf_op jit(solution)/shard_map/all_gather | solution.py:568
  130.0 0.6 slice.12
  130.8 0.5 add_bitcast_fusion
  (16 shorter events, 0.2 us)
Async XLA Ops:
  0.6 14.4 %collective-permute-start = (bf16[768,1536]{1,0:T(8,128)(2,1)}, bf16[768,1536]{1,0:T(8,128)(2,1)}, u32[]{:S(2)}, u32[]{:S(2)}) collective-permute-start(bf16[768,1536]{1,0:T(8,128)(2,1)} %up_a_hbm.3), channel_id=1, source_target_pairs={{0,1},{1,0},{2,3},{3,2},{4,5},{5,4},{6,7},{7,6},{8,9},{9,8},{10,11... | collective-permute-start | bytes 7077896 | tf_op jit(solution)/shard_map/ppermute | solution.py:534
  3.9 11.1 %collective-permute-start.1 = (bf16[1536,768]{1,0:T(8,128)(2,1)}, bf16[1536,768]{1,0:T(8,128)(2,1)}, u32[]{:S(2)}, u32[]{:S(2)}) collective-permute-start(bf16[1536,768]{1,0:T(8,128)(2,1)} %down_a_hbm.3), channel_id=1, source_target_pairs={{0,1},{1,0},{2,3},{3,2},{4,5},{5,4},{6,7},{7,6},{8,9},{9,8},{10,11... | collective-permute-start | bytes 7077896 | tf_op jit(solution)/shard_map/ppermute | solution.py:535
  8.2 6.2 %copy-start = (f32[1,16384]{1,0:T(1,128)S(1)}, f32[1,16384]{1,0:T(1,128)}, u32[]{:S(2)}) copy-start(f32[1,16384]{1,0:T(1,128)} %param.20) | copy-start | bytes 196612
  15.1 38.2 %copy-start.4 = (s32[4]{0:T(128)S(1)}, s32[4]{0:T(128)}, u32[]{:S(2)}) copy-start(s32[4]{0:T(128)} %pad_add_fusion.where_ref) | copy-start | bytes 52
  70.0 0.8 copy-start.2
  71.3 0.6 copy-start.1
  76.7 36.8 %copy-start.5 = (s32[4]{0:T(128)S(1)}, s32[4]{0:T(128)}, u32[]{:S(2)}) copy-start(s32[4]{0:T(128)} %pad_add_fusion.where_ref) | copy-start | bytes 52
  76.7 47.7 %copy-start.6 = (f32[2,1]{1,0:T(2,128)S(1)}, f32[2,1]{1,0:T(2,128)}, u32[]{:S(2)}) copy-start(f32[2,1]{1,0:T(2,128)} %copy.26.mixing_ref) | copy-start | bytes 28
  124.4 0.8 copy-start.3

commit v2 on v1

--- a/solution.py
+++ b/solution.py
@@ -27,10 +27,12 @@
 PER_ROW = LANES // PATCH
 DENSE = OWN // PER_ROW
 HALF = D // 2
-ROWS = 256
+ROWS = 512
 GROUPS = ROWS // DENSE
 MLP_ROWS = 512
 MLP_CHUNK = 768
+EMBED_ROWS = 512
+EMBED_GROUPS = EMBED_ROWS // DENSE
 MIB = 1 << 20
 EXTRA = 8
 FULL = DENSE + EXTRA
@@ -87,7 +89,6 @@
     where_ref,
     timesteps_ref,
     label_ref,
-    noise_ref,
     logs_hbm,
     table_hbm,
     class_hbm,
@@ -97,7 +98,6 @@
     final_ada_hbm,
     modul_ref,
     coef_ref,
-    tokens_ref,
     logs,
     table,
     class_rows,
@@ -125,7 +125,6 @@
         )
     for copy in copies:
         copy.start()
-    tokens_ref[...] = noise_ref[...].astype(jnp.bfloat16)
     point = where_ref[3]
     now, after = timesteps_ref[point], timesteps_ref[point + 1]
 
@@ -168,16 +167,15 @@
         modul_ref[:, column * D : (column + 1) * D] = matmul(summed, ada[column])
 
 
-def condition(where, timesteps, labels, noise, *weights):
+def condition(where, timesteps, labels, *weights):
     return pl.pallas_call(
         condition_kernel,
         out_shape=(
             jax.ShapeDtypeStruct((1, 8 * D), jnp.float32),
             jax.ShapeDtypeStruct((16, LANES), jnp.float32),
-            jax.ShapeDtypeStruct((2 * DENSE, LANES), jnp.bfloat16),
         ),
-        in_specs=[SMEM] * 3 + [VMEM] + [HBM] * 7,
-        out_specs=(VMEM, VMEM, VMEM),
+        in_specs=[SMEM] * 3 + [HBM] * 7,
+        out_specs=(VMEM, VMEM),
         scratch_shapes=[
             pltpu.VMEM((8, LANES), jnp.float32),
             pltpu.VMEM((2 * STEP, FREQ), jnp.float32),
@@ -189,13 +187,12 @@
         ],
         compiler_params=pltpu.CompilerParams(vmem_limit_bytes=62 * MIB),
         name="condition",
-    )(where, timesteps, labels, noise, log_table(), time_table(), *weights)
+    )(where, timesteps, labels, log_table(), time_table(), *weights)
 
 
 def denoise_kernel(
     where_ref,
     mixing_ref,
-    tokens_ref,
     state_ref,
     modul_ref,
     coef_ref,
@@ -210,7 +207,6 @@
     down_a_hbm,
     up_b_hbm,
     down_b_hbm,
-    drift_ref,
     payload_ref,
     coarse_w,
     fine_w,
@@ -252,7 +248,7 @@
     def embedded(dense, coarse, first_group):
         coarse_sin, coarse_cos = coarse[:, :HALF], coarse[:, HALF:]
         pieces = []
-        for group in range(first_group, first_group + GROUPS):
+        for group in range(first_group, first_group + EMBED_GROUPS):
             picked = jnp.where(dense_lane == group, dense, jnp.zeros_like(dense))
             fine_sin = fine_w[group : group + 1, 0:HALF]
             fine_cos = fine_w[group : group + 1, HALF:D]
@@ -268,11 +264,11 @@
 
     for half in range(2):
         start = pl.multiple_of((member if half == 0 else 1 - member) * DENSE, DENSE)
-        dense = tokens_ref[pl.ds(start, DENSE), :]
+        dense = state_ref[pl.ds(start, DENSE), :].astype(jnp.bfloat16)
         coarse = coarse_w[pl.ds(start, DENSE), :]
-        for block in range(OWN // ROWS):
-            low = block * ROWS
-            hidden = embedded(dense, coarse, block * GROUPS)
+        for block in range(OWN // EMBED_ROWS):
+            low = block * EMBED_ROWS
+            hidden = embedded(dense, coarse, block * EMBED_GROUPS)
             attn_in = normed(hidden, shift_attn, scale_attn).astype(jnp.bfloat16)
             if half == 0 and block == 0:
                 copies[3].wait()
@@ -280,16 +276,16 @@
                 for copy in copies[5:]:
                     copy.start()
             if half == 0:
-                hidden_all[low : low + ROWS, :] = hidden
+                hidden_all[low : low + EMBED_ROWS, :] = hidden
                 q = (matmul(attn_in, q_w[...]) * Q_FACTOR).astype(jnp.bfloat16)
                 for pair in range(PAIRS):
-                    queries[pair, low : low + ROWS, :] = q[:, pair * LANES : (pair + 1) * LANES]
+                    queries[pair, low : low + EMBED_ROWS, :] = q[:, pair * LANES : (pair + 1) * LANES]
             both = matmul(attn_in, kv_w[...]).astype(jnp.bfloat16)
             at = half * OWN + low
             for pair in range(PAIRS):
                 here = pair * LANES
-                keys[pair, at : at + ROWS, :] = both[:, here : here + LANES]
-                values[pair, at : at + ROWS, 0:LANES] = both[:, D + here : D + here + LANES]
+                keys[pair, at : at + EMBED_ROWS, :] = both[:, here : here + LANES]
+                values[pair, at : at + EMBED_ROWS, 0:LANES] = both[:, D + here : D + here + LANES]
 
     lane = lax.broadcasted_iota(jnp.int32, (ROWS, LANES), 1)
 
@@ -308,31 +304,20 @@
 
     def over_pair(pair, carry):
         score(pair, 0, 1, 1)
-        outs = [weigh(pair, 0)]
-        score(pair, 1, 0, 0)
-        outs.append(weigh(pair, 1))
-        score(pair, 1, 1, 1)
-        outs.append(weigh(pair, 0))
+        even = weigh(pair, 0)
         score(jnp.minimum(pair + 1, PAIRS - 1), 0, 0, 0)
-        outs.append(weigh(pair, 1))
+        odd = weigh(pair, 1)
         at = pl.multiple_of(pair * LANES, LANES)
-        for block in range(OWN // ROWS):
-            attended[block * ROWS : (block + 1) * ROWS, pl.ds(at, LANES)] = jnp.where(
-                lane < LANES // 2, outs[2 * block], outs[2 * block + 1]
-            ).astype(jnp.bfloat16)
+        attended[:, pl.ds(at, LANES)] = jnp.where(lane < LANES // 2, even, odd).astype(jnp.bfloat16)
         return carry
 
     score(0, 0, 0, 0)
     lax.fori_loop(0, PAIRS, over_pair, 0)
 
     eps = jnp.zeros((DENSE, LANES), jnp.float32)
-    chosen = (
-        lax.broadcasted_iota(jnp.int32, (PATCH, LANES), 1) % PATCH
-        == lax.broadcasted_iota(jnp.int32, (PATCH, LANES), 0)
-    ).astype(jnp.bfloat16)
     copies[5].wait()
     copies[6].wait()
-    final_tiled = matmul(final_w[...], chosen).astype(jnp.bfloat16)
+    final_tiled = jnp.concatenate([final_w[...]] * PER_ROW, axis=0)
     for copy in copies[7:]:
         copy.wait()
     for block in range(OWN // MLP_ROWS):
@@ -357,15 +342,17 @@
         mlp_out = sum(share.astype(jnp.bfloat16).astype(jnp.float32) for share in shares)
         h2 = h1 + gate_mlp * mlp_out
         final_in = normed(h2, shift_out, scale_out).astype(jnp.bfloat16)
-        predicted = matmul(final_in, final_tiled)
+        predicted = lax.dot_general(
+            final_in, final_tiled, (((1,), (1,)), ((), ())), preferred_element_type=jnp.float32
+        )
         for group in range(MLP_ROWS // DENSE):
             eps = jnp.where(
                 dense_lane == block * (MLP_ROWS // DENSE) + group,
                 predicted[group * DENSE : (group + 1) * DENSE, :],
                 eps,
             )
-    drift = coef_ref[0:1, :] * state_ref[...] + coef_ref[8:9, :] * eps
-    drift_ref[...] = drift
+    own = state_ref[pl.ds(pl.multiple_of(member * DENSE, DENSE), DENSE), :]
+    drift = coef_ref[0:1, :] * own + coef_ref[8:9, :] * eps
     mixing = jnp.full((EXTRA, LANES), mixing_ref[0, 0], jnp.float32)
     rounded = mixing.astype(jnp.bfloat16).astype(jnp.float32)
     row = lax.broadcasted_iota(jnp.int32, (EXTRA, LANES), 0)
@@ -375,16 +362,13 @@
         payload_ref[copy] = sent
 
 
-def denoise(copies, where, mixing, tokens, state, modul, coefs, *weights):
+def denoise(copies, where, mixing, state, modul, coefs, *weights):
     bf16 = jnp.bfloat16
     return pl.pallas_call(
         denoise_kernel,
-        out_shape=(
-            jax.ShapeDtypeStruct((DENSE, LANES), jnp.float32),
-            jax.ShapeDtypeStruct((copies, FULL, LANES), bf16),
-        ),
-        in_specs=[SMEM] * 2 + [VMEM] * 4 + [HBM] * 11,
-        out_specs=(VMEM, VMEM),
+        out_shape=jax.ShapeDtypeStruct((copies, FULL, LANES), bf16),
+        in_specs=[SMEM] * 2 + [VMEM] * 3 + [HBM] * 11,
+        out_specs=VMEM,
         scratch_shapes=[
             pltpu.VMEM((SEQ // PER_ROW, D), jnp.float32),
             pltpu.VMEM((PER_ROW, D), jnp.float32),
@@ -392,7 +376,7 @@
             pltpu.VMEM((D, 2 * D), bf16),
             pltpu.VMEM((D, D), bf16),
             pltpu.VMEM((D, D), bf16),
-            pltpu.VMEM((D, PATCH), bf16),
+            pltpu.VMEM((PATCH, D), bf16),
             pltpu.VMEM((2, D, FF_OWN), bf16),
             pltpu.VMEM((2, FF_OWN, D), bf16),
             pltpu.VMEM((OWN, D), jnp.float32),
@@ -405,7 +389,7 @@
         ],
         compiler_params=pltpu.CompilerParams(vmem_limit_bytes=61 * MIB),
         name="denoise",
-    )(where, mixing, tokens, state, modul, coefs, *weights)
+    )(where, mixing, state, modul, coefs, *weights)
 
 
 def plane_kernel(where_ref, pieces_ref, inside_ref, payload_ref):
@@ -413,14 +397,17 @@
     count = pieces_ref.shape[0]
     before = jnp.zeros((DENSE, LANES), jnp.float32)
     total = before
+    own = before
     beside = jnp.zeros((EXTRA, LANES), jnp.float32)
     for k in range(count):
         piece = pieces_ref[k].astype(jnp.float32)
         before = before + jnp.where(k < here, piece[:DENSE], 0.0)
+        own = jnp.where(k == here, piece[:DENSE], own)
         total = total + piece[:DENSE]
         beside = jnp.where(k == here - 1, piece[DENSE:], beside)
     inside_ref[0:DENSE, :] = before
     inside_ref[DENSE:FULL, :] = beside
+    inside_ref[FULL:, :] = own
     last = pieces_ref[count - 1, DENSE:FULL, :].astype(jnp.float32)
     sent = jnp.concatenate([total, last], axis=0).astype(jnp.bfloat16)
     for copy in range(payload_ref.shape[0]):
@@ -431,7 +418,7 @@
     return pl.pallas_call(
         plane_kernel,
         out_shape=(
-            jax.ShapeDtypeStruct((FULL, LANES), jnp.float32),
+            jax.ShapeDtypeStruct((FULL + DENSE, LANES), jnp.float32),
             jax.ShapeDtypeStruct((planes, FULL, LANES), jnp.bfloat16),
         ),
         in_specs=[SMEM, VMEM],
@@ -450,41 +437,39 @@
 
 
 def advance_kernel(
-    where_ref, planes_ref, inside_ref, drift_ref, noise_ref, reached_ref, state_ref, tokens_ref
+    where_ref, planes_ref, inside_ref, noise_ref, reached_ref, state_ref
 ):
     before = entered(where_ref, planes_ref, inside_ref)
-    reached_ref[...] = before + drift_ref[...]
+    reached_ref[...] = before + inside_ref[FULL:, :]
     beside = inside_ref[DENSE:FULL, :]
     for k in range(planes_ref.shape[0]):
         found = jnp.logical_and(where_ref[1] == 0, k == where_ref[2] - 1)
         beside = jnp.where(found, planes_ref[k, DENSE:FULL, :].astype(jnp.float32), beside)
     mixing = jnp.sum(beside, axis=0, keepdims=True)
     start = pl.multiple_of(where_ref[0] * DENSE, DENSE)
-    state = noise_ref[pl.ds(start, DENSE), :] + (1.0 + mixing) * before
-    state_ref[...] = state
-    tokens_ref[...] = state.astype(jnp.bfloat16)
-
-
-def advance(where, planes, inside, drift, noise):
+    state_ref[...] = noise_ref[pl.ds(start, DENSE), :] + (1.0 + mixing) * before
+
+
+def advance(where, planes, inside, noise):
     field = jax.ShapeDtypeStruct((DENSE, LANES), jnp.float32)
     return pl.pallas_call(
         advance_kernel,
-        out_shape=(field, field, jax.ShapeDtypeStruct((DENSE, LANES), jnp.bfloat16)),
-        in_specs=[SMEM] + [VMEM] * 4,
-        out_specs=(VMEM, VMEM, VMEM),
+        out_shape=(field, field),
+        in_specs=[SMEM] + [VMEM] * 3,
+        out_specs=(VMEM, VMEM),
         compiler_params=pltpu.CompilerParams(vmem_limit_bytes=8 * MIB),
         name="advance",
-    )(where, planes, inside, drift, noise)
+    )(where, planes, inside, noise)
 
 
 def close_kernel(
-    where_ref, mixing_ref, planes_ref, inside_ref, drift_ref, noise_ref, first_ref, packed_ref
+    where_ref, mixing_ref, planes_ref, inside_ref, noise_ref, first_ref, packed_ref
 ):
-    reached = entered(where_ref, planes_ref, inside_ref) + drift_ref[...]
+    reached = entered(where_ref, planes_ref, inside_ref) + inside_ref[FULL:, :]
     first = first_ref[...]
     start = pl.multiple_of(where_ref[0] * DENSE, DENSE)
     packed_ref[0:DENSE, :] = (
-        noise_ref[pl.ds(start, DENSE), :] + reached + mixing_ref[1, 0] * (reached - first)
+        noise_ref[pl.ds(start, DENSE), :] + reached + mixing_ref[0, 1] * (reached - first)
     )
     missed = reached - (1.0 + mixing_ref[0, 0]) * first
 
@@ -497,15 +482,15 @@
     )
 
 
-def close(where, mixing, planes, inside, drift, noise, first):
+def close(where, mixing, planes, inside, noise, first):
     return pl.pallas_call(
         close_kernel,
         out_shape=jax.ShapeDtypeStruct((FULL, LANES), jnp.float32),
-        in_specs=[SMEM] * 2 + [VMEM] * 5,
+        in_specs=[SMEM] * 2 + [VMEM] * 4,
         out_specs=VMEM,
         compiler_params=pltpu.CompilerParams(vmem_limit_bytes=8 * MIB),
         name="close",
-    )(where, mixing, planes, inside, drift, noise, first)
+    )(where, mixing, planes, inside, noise, first)
 
 
 def exchanged(copies, axis):
@@ -537,11 +522,10 @@
         [lax.axis_index(axis) for axis in ("tensor", PLANE, "tm_0", TM)]
     ).astype(jnp.int32)
     noise = noise_start.reshape(2 * DENSE, LANES)
-    modul, coefs, tokens = condition(
+    modul, coefs = condition(
         where,
         timesteps,
         class_labels,
-        noise,
         class_table,
         time_in,
         time_out,
@@ -549,25 +533,22 @@
         final_ada,
     )
     coarse, fine = place_tables()
-    weights = (coarse, fine, patch_weight, kv_weight, q_weight, out_weight, final_weight)
+    weights = (coarse, fine, patch_weight, kv_weight, q_weight, out_weight, final_weight.T)
     weights += (up_weight, down_weight, up_other, down_other)
 
-    def scanned(tokens, state):
-        drift, payload = denoise(
-            lax.axis_size(PLANE), where, mixing, tokens, state, modul, coefs, *weights
-        )
+    mixing = mixing.T
+
+    def scanned(state):
+        payload = denoise(lax.axis_size(PLANE), where, mixing, state, modul, coefs, *weights)
         pieces = exchanged(payload, PLANE)
         inside, payload = plane(where, pieces, lax.axis_size("tm_0"))
-        return drift, inside, exchanged(payload, "tm_0")
-
-    noise_own = lax.dynamic_slice_in_dim(noise, where[0] * DENSE, DENSE, 0)
-    drift, inside, planes = scanned(tokens, noise_own)
-    reached, state, tokens = advance(where, planes, inside, drift, noise)
-    tokens = lax.all_gather(tokens, "tensor", tiled=True)
-    drift, inside, planes = scanned(tokens, state)
-    packed = lax.all_gather(
-        close(where, mixing, planes, inside, drift, noise, reached), "tensor"
-    )
+        return inside, exchanged(payload, "tm_0")
+
+    inside, planes = scanned(noise)
+    reached, state = advance(where, planes, inside, noise)
+    state = lax.all_gather(state, "tensor", tiled=True)
+    inside, planes = scanned(state)
+    packed = lax.all_gather(close(where, mixing, planes, inside, noise, reached), "tensor")
     states = packed[:, :DENSE].reshape(1, 1, 2 * DENSE * LANES)
     residuals = packed[0, DENSE : DENSE + ITERS, :1] + packed[1, DENSE : DENSE + ITERS, :1]
     return (states, residuals)

time: 132 us -> 125 us (0.947)
  local copies, waits for them, and re-layouts: 6.45 us -> 0.83 us
  Pallas kernels: 57.9 us -> 56.5 us
    unnamed x18 -> x10, local copies, waits for them, and re-layouts: 5.2 us -> 0.2 us
  transfers between devices with their start and end apart: 2 -> 2, of which waited for: 0 -> 1; matrix products, arithmetic and copies ran while one was open for 3% -> 1% of each run, Pallas kernels for 5% -> 5%
where the time goes in v2:
time: 125 us
  blocking collectives  61.1 us (49%)
  Pallas kernels  56.5 us (45%)
  starting transfers between devices  3.39 us (3%)
  between operations  1.35 us (1%)
    all_to_all x4, blocking collectives, exchanged(): return lax.all_to_all(copies, axis, split_axis=0, concat_axis=0, tiled=True)  52.2 us
    pallas_call x2, Pallas kernels, denoise(): pl.pallas_call(denoise_kernel, out_shape=jax.ShapeDtypeStruct((copies, FU...  48 us
    pallas_call x1, Pallas kernels, condition(): pl.pallas_call(condition_kernel, out_shape=(jax.ShapeDtypeStruct((1, 8 *...  6.01 us
    all_gather x1, blocking collectives, per_device(): state = lax.all_gather(state, 'tensor', tiled=True)  4.78 us
    all_gather x1, blocking collectives, per_device(): lax.all_gather(close(where, mixing, planes, inside, noise, reached), 'ten...  4.07 us
    ppermute x1, starting transfers between devices, per_device(): up_other = lax.ppermute(up_weight, 'tensor', swap)  3.29 us
  transfers between devices with their start and end apart: 2, of which 1 were waited for; matrix products, arithmetic and copies ran while one was open for 1% of the time, Pallas kernels for 5%

profile of v2, /device:TPU:1, one launch (start us, length us, event | category | flops | bytes accessed | tf_op | source)
XLA Modules:
  0.0 124.8 jit_solution(4779113887799558320)
XLA Ops:
  0.6 3.3 %collective-permute-start = (bf16[768,1536]{1,0:T(8,128)(2,1)}, bf16[768,1536]{1,0:T(8,128)(2,1)}, u32[]{:S(2)}, u32[]{:S(2)}) collective-permute-start(bf16[768,1536]{1,0:T(8,128)(2,1)} %up_a_hbm.3), channel_id=1, source_target_pairs={{0,1},{1,0},{2,3},{3,2},{4,5},{5,4},{6,7},{7,6},{8,9},{9,8},{10,11... | collective-permute-start | bytes 7077896 | tf_op jit(solution)/shard_map/ppermute | solution.py:519
  3.9 0.1 collective-permute-start.1
  4.7 0.7 pad_add_fusion.where_ref
  5.3 6.0 %condition.1 = (f32[1,6144]{1,0:T(1,128)}, f32[16,128]{1,0:T(8,128)}) custom-call(s32[4]{0:T(128)} %pad_add_fusion.where_ref, s32[129]{0:T(256)} %timesteps_ref.1, s32[1,1]{1,0:T(1,128)S(6)} %copy.26.label_ref, f32[8,128]{1,0:T(8,128)} %constant.28.clone.logs_hbm, f32[64,256]{1,0:T(8,128)} %constant.29.clone.table_hbm, bf16[1000,768]{1,0:T(8,128)(2,1)} %class_hbm.1, ...), custom_call_target="tpu_custom_call" | custom-call | tf_op jit(solution)/shard_map/condition/pallas_call | solution.py:171
  11.4 0.0 collective-permute-done.up_b_hbm
  11.4 0.4 collective-permute-done.1.down_b_hbm
  11.8 24.1 %denoise.2 = bf16[16,72,128]{2,1,0:T(8,128)(2,1)} custom-call(s32[4]{0:T(128)} %pad_add_fusion.where_ref, f32[1,2]{1,0:T(1,128)} %bitcast.14, f32[128,128]{1,0:T(8,128)} %bitcast.11, f32[1,6144]{1,0:T(1,128)} %get-tuple-element.10.modul_ref, f32[16,128]{1,0:T(8,128)} %get-tuple-element.11.coef_ref, f32[128,768]{1,0:T(8,128)} %constant.30.clone.coarse_hbm, ...), custom_call_target="tpu_custom_call" | custom-call | tf_op jit(solution)/shard_map/denoise/pallas_call | solution.py:367
  35.9 13.5 %all_to_all.20.pieces_ref = bf16[16,72,128]{2,1,0:T(8,128)(2,1)S(1)} all-to-all(bf16[16,72,128]{2,1,0:T(8,128)(2,1)} %denoise.2), channel_id=1, replica_groups=mesh['tm_0'=8,'tm_1'=4,'tm_2'=4,'tensor'=2] {'tm_1','tm_2'}, dimensions={0} | all-to-all | bytes 589824 | tf_op jit(solution)/shard_map/all_to_all | solution.py:497
  49.4 0.0 copy-done.1
  49.4 0.7 plane.2
  50.1 16.1 %all_to_all.21.planes_ref = bf16[8,72,128]{2,1,0:T(8,128)(2,1)S(1)} all-to-all(bf16[8,72,128]{2,1,0:T(8,128)(2,1)S(1)} %get-tuple-element.12), channel_id=1, replica_groups=mesh['tm_0'=8,'tm_1'=4,'tm_2'=4,'tensor'=2] {'tm_0'}, dimensions={0} | all-to-all | bytes 294912 | tf_op jit(solution)/shard_map/all_to_all | solution.py:497
  66.2 0.0 copy-done
  66.2 0.6 advance.1
  66.8 4.8 %all_gather.9.state_ref = f32[128,128]{1,0:T(8,128)} all-gather(f32[64,128]{1,0:T(8,128)S(1)} %get-tuple-element.14), channel_id=1, replica_groups=mesh['tm_0'=8,'tm_1'=4,'tm_2'=4,'tensor'=2] {'tensor'}, dimensions={0}, use_global_device_ids=true | all-gather | bytes 98304 | tf_op jit(solution)/shard_map/all_gather | solution.py:549
  71.6 23.9 %denoise.3 = bf16[16,72,128]{2,1,0:T(8,128)(2,1)} custom-call(s32[4]{0:T(128)} %pad_add_fusion.where_ref, f32[1,2]{1,0:T(1,128)} %bitcast.15, f32[128,128]{1,0:T(8,128)} %all_gather.9.state_ref, f32[1,6144]{1,0:T(1,128)} %get-tuple-element.10.modul_ref, f32[16,128]{1,0:T(8,128)} %get-tuple-element.11.coef_ref, f32[128,768]{1,0:T(8,128)} %constant.30.clone.coarse_hbm, ...), custom_call_target="tpu_custom_call" | custom-call | tf_op jit(solution)/shard_map/denoise/pallas_call | solution.py:367
  95.4 12.3 %all_to_all.22.pieces_ref = bf16[16,72,128]{2,1,0:T(8,128)(2,1)S(1)} all-to-all(bf16[16,72,128]{2,1,0:T(8,128)(2,1)} %denoise.3), channel_id=1, replica_groups=mesh['tm_0'=8,'tm_1'=4,'tm_2'=4,'tensor'=2] {'tm_1','tm_2'}, dimensions={0} | all-to-all | bytes 589824 | tf_op jit(solution)/shard_map/all_to_all | solution.py:497
  107.7 0.7 plane.3
  108.4 10.3 %all_to_all.23.planes_ref = bf16[8,72,128]{2,1,0:T(8,128)(2,1)S(1)} all-to-all(bf16[8,72,128]{2,1,0:T(8,128)(2,1)S(1)} %get-tuple-element.15), channel_id=1, replica_groups=mesh['tm_0'=8,'tm_1'=4,'tm_2'=4,'tensor'=2] {'tm_0'}, dimensions={0} | all-to-all | bytes 294912 | tf_op jit(solution)/shard_map/all_to_all | solution.py:497
  118.7 0.7 close.1
  119.4 4.1 %all-gather = f32[144,128]{1,0:T(8,128)S(1)} all-gather(f32[72,128]{1,0:T(8,128)S(1)} %close.1), channel_id=2, replica_groups=mesh['tm_0'=8,'tm_1'=4,'tm_2'=4,'tensor'=2] {'tensor'}, dimensions={0}, use_global_device_ids=true | all-gather | bytes 110592 | tf_op jit(solution)/shard_map/all_gather | solution.py:551
  123.4 0.6 slice.12
  124.1 0.1 copy.25
  124.2 0.1 copy.24
  124.2 0.5 add_bitcast_fusion
  (7 shorter events, 0.0 us)
Async XLA Ops:
  0.6 10.7 %collective-permute-start = (bf16[768,1536]{1,0:T(8,128)(2,1)}, bf16[768,1536]{1,0:T(8,128)(2,1)}, u32[]{:S(2)}, u32[]{:S(2)}) collective-permute-start(bf16[768,1536]{1,0:T(8,128)(2,1)} %up_a_hbm.3), channel_id=1, source_target_pairs={{0,1},{1,0},{2,3},{3,2},{4,5},{5,4},{6,7},{7,6},{8,9},{9,8},{10,11... | collective-permute-start | bytes 7077896 | tf_op jit(solution)/shard_map/ppermute | solution.py:519
  3.9 7.9 %collective-permute-start.1 = (bf16[1536,768]{1,0:T(8,128)(2,1)}, bf16[1536,768]{1,0:T(8,128)(2,1)}, u32[]{:S(2)}, u32[]{:S(2)}) collective-permute-start(bf16[1536,768]{1,0:T(8,128)(2,1)} %down_a_hbm.3), channel_id=1, source_target_pairs={{0,1},{1,0},{2,3},{3,2},{4,5},{5,4},{6,7},{7,6},{8,9},{9,8},{10,11... | collective-permute-start | bytes 7077896 | tf_op jit(solution)/shard_map/ppermute | solution.py:520
  11.8 37.6 %copy-start.1 = (s32[4]{0:T(128)S(1)}, s32[4]{0:T(128)}, u32[]{:S(2)}) copy-start(s32[4]{0:T(128)} %pad_add_fusion.where_ref) | copy-start | bytes 52
  11.8 54.4 %copy-start = (f32[1,16384]{1,0:T(1,128)S(1)}, f32[1,16384]{1,0:T(1,128)}, u32[]{:S(2)}) copy-start(f32[1,16384]{1,0:T(1,128)} %param.20) | copy-start | bytes 196612
  71.6 36.2 %copy-start.2 = (s32[4]{0:T(128)S(1)}, s32[4]{0:T(128)}, u32[]{:S(2)}) copy-start(s32[4]{0:T(128)} %pad_add_fusion.where_ref) | copy-start | bytes 52
  71.6 47.1 %copy-start.3 = (f32[2,1]{0,1:T(1,128)S(1)}, f32[2,1]{0,1:T(1,128)}, u32[]{:S(2)}) copy-start(f32[2,1]{0,1:T(1,128)} %param.23) | copy-start | bytes 28

commit v3 on v2

--- a/solution.py
+++ b/solution.py
@@ -302,17 +302,21 @@
         o = matmul(e, values[pair])
         return o[:, :LANES] / o[:, LANES:]
 
-    def over_pair(pair, carry):
+    def over_pair(pair):
         score(pair, 0, 1, 1)
         even = weigh(pair, 0)
         score(jnp.minimum(pair + 1, PAIRS - 1), 0, 0, 0)
         odd = weigh(pair, 1)
         at = pl.multiple_of(pair * LANES, LANES)
         attended[:, pl.ds(at, LANES)] = jnp.where(lane < LANES // 2, even, odd).astype(jnp.bfloat16)
+
+    def over_pairs(step, carry):
+        for inner in range(2):
+            over_pair(2 * step + inner)
         return carry
 
     score(0, 0, 0, 0)
-    lax.fori_loop(0, PAIRS, over_pair, 0)
+    lax.fori_loop(0, PAIRS // 2, over_pairs, 0)
 
     eps = jnp.zeros((DENSE, LANES), jnp.float32)
     copies[5].wait()
@@ -550,7 +554,7 @@
     inside, planes = scanned(state)
     packed = lax.all_gather(close(where, mixing, planes, inside, noise, reached), "tensor")
     states = packed[:, :DENSE].reshape(1, 1, 2 * DENSE * LANES)
-    residuals = packed[0, DENSE : DENSE + ITERS, :1] + packed[1, DENSE : DENSE + ITERS, :1]
+    residuals = jnp.sum(packed[:, DENSE : DENSE + ITERS, :1], axis=0)
     return (states, residuals)
 
 

time: 125 us -> 124 us (level)
  transfers between devices with their start and end apart: 2 -> 2, of which waited for: 1 -> 1; matrix products, arithmetic and copies ran while one was open for 1% -> 0% of each run, Pallas kernels for 5% -> 5%
where the time goes in v3:
time: 124 us
  blocking collectives  60.8 us (49%)
  Pallas kernels  55.8 us (45%)
  starting transfers between devices  3.39 us (3%)
  between operations  1.35 us (1%)
  other arithmetic  1.24 us (1%)
    all_to_all x4, blocking collectives, exchanged(): return lax.all_to_all(copies, axis, split_axis=0, concat_axis=0, tiled=True)  52.2 us
    pallas_call x2, Pallas kernels, denoise(): pl.pallas_call(denoise_kernel, out_shape=jax.ShapeDtypeStruct((copies, FU...  47.2 us
    pallas_call x1, Pallas kernels, condition(): pl.pallas_call(condition_kernel, out_shape=(jax.ShapeDtypeStruct((1, 8 *...  6.01 us
    all_gather x1, blocking collectives, per_device(): state = lax.all_gather(state, 'tensor', tiled=True)  4.56 us
    all_gather x1, blocking collectives, per_device(): lax.all_gather(close(where, mixing, planes, inside, noise, reached), 'ten...  4.07 us
    ppermute x1, starting transfers between devices, per_device(): up_other = lax.ppermute(up_weight, 'tensor', swap)  3.29 us
  transfers between devices with their start and end apart: 2, of which 1 were waited for; matrix products, arithmetic and copies ran while one was open for 0% of the time, Pallas kernels for 5%

profile of v3, /device:TPU:1, one launch (start us, length us, event | category | flops | bytes accessed | tf_op | source)
XLA Modules:
  0.0 123.7 jit_solution(352193395654184409)
XLA Ops:
  0.6 3.3 %collective-permute-start = (bf16[768,1536]{1,0:T(8,128)(2,1)}, bf16[768,1536]{1,0:T(8,128)(2,1)}, u32[]{:S(2)}, u32[]{:S(2)}) collective-permute-start(bf16[768,1536]{1,0:T(8,128)(2,1)} %up_a_hbm.3), channel_id=1, source_target_pairs={{0,1},{1,0},{2,3},{3,2},{4,5},{5,4},{6,7},{7,6},{8,9},{9,8},{10,11... | collective-permute-start | bytes 7077896 | tf_op jit(solution)/shard_map/ppermute | solution.py:523
  3.9 0.1 collective-permute-start.1
  4.7 0.6 pad_add_fusion.where_ref
  5.3 6.0 %condition.1 = (f32[1,6144]{1,0:T(1,128)}, f32[16,128]{1,0:T(8,128)}) custom-call(s32[4]{0:T(128)} %pad_add_fusion.where_ref, s32[129]{0:T(256)} %timesteps_ref.1, s32[1,1]{1,0:T(1,128)S(6)} %copy.22.label_ref, f32[8,128]{1,0:T(8,128)} %constant.30.clone.logs_hbm, f32[64,256]{1,0:T(8,128)} %constant.31.clone.table_hbm, bf16[1000,768]{1,0:T(8,128)(2,1)} %class_hbm.1, ...), custom_call_target="tpu_custom_call" | custom-call | tf_op jit(solution)/shard_map/condition/pallas_call | solution.py:171
  11.3 0.0 collective-permute-done.up_b_hbm
  11.3 0.5 collective-permute-done.1.down_b_hbm
  11.8 23.6 %denoise.2 = bf16[16,72,128]{2,1,0:T(8,128)(2,1)} custom-call(s32[4]{0:T(128)} %pad_add_fusion.where_ref, f32[1,2]{1,0:T(1,128)} %bitcast.13, f32[128,128]{1,0:T(8,128)} %bitcast.10, f32[1,6144]{1,0:T(1,128)} %get-tuple-element.10.modul_ref, f32[16,128]{1,0:T(8,128)} %get-tuple-element.11.coef_ref, f32[128,768]{1,0:T(8,128)} %constant.32.clone.coarse_hbm, ...), custom_call_target="tpu_custom_call" | custom-call | tf_op jit(solution)/shard_map/denoise/pallas_call | solution.py:371
  35.4 13.5 %all_to_all.20.pieces_ref = bf16[16,72,128]{2,1,0:T(8,128)(2,1)S(1)} all-to-all(bf16[16,72,128]{2,1,0:T(8,128)(2,1)} %denoise.2), channel_id=1, replica_groups=mesh['tm_0'=8,'tm_1'=4,'tm_2'=4,'tensor'=2] {'tm_1','tm_2'}, dimensions={0} | all-to-all | bytes 589824 | tf_op jit(solution)/shard_map/all_to_all | solution.py:501
  49.0 0.0 copy-done.1
  49.0 0.7 plane.2
  49.6 16.1 %all_to_all.21.planes_ref = bf16[8,72,128]{2,1,0:T(8,128)(2,1)S(1)} all-to-all(bf16[8,72,128]{2,1,0:T(8,128)(2,1)S(1)} %get-tuple-element.12), channel_id=1, replica_groups=mesh['tm_0'=8,'tm_1'=4,'tm_2'=4,'tensor'=2] {'tm_0'}, dimensions={0} | all-to-all | bytes 294912 | tf_op jit(solution)/shard_map/all_to_all | solution.py:501
  65.7 0.0 copy-done
  65.7 0.6 advance.1
  66.3 4.6 %all_gather.9.state_ref = f32[128,128]{1,0:T(8,128)} all-gather(f32[64,128]{1,0:T(8,128)S(1)} %get-tuple-element.14), channel_id=1, replica_groups=mesh['tm_0'=8,'tm_1'=4,'tm_2'=4,'tensor'=2] {'tensor'}, dimensions={0}, use_global_device_ids=true | all-gather | bytes 98304 | tf_op jit(solution)/shard_map/all_gather | solution.py:553
  70.9 23.6 %denoise.3 = bf16[16,72,128]{2,1,0:T(8,128)(2,1)} custom-call(s32[4]{0:T(128)} %pad_add_fusion.where_ref, f32[1,2]{1,0:T(1,128)} %bitcast.14, f32[128,128]{1,0:T(8,128)} %all_gather.9.state_ref, f32[1,6144]{1,0:T(1,128)} %get-tuple-element.10.modul_ref, f32[16,128]{1,0:T(8,128)} %get-tuple-element.11.coef_ref, f32[128,768]{1,0:T(8,128)} %constant.32.clone.coarse_hbm, ...), custom_call_target="tpu_custom_call" | custom-call | tf_op jit(solution)/shard_map/denoise/pallas_call | solution.py:371
  94.5 12.3 %all_to_all.22.pieces_ref = bf16[16,72,128]{2,1,0:T(8,128)(2,1)S(1)} all-to-all(bf16[16,72,128]{2,1,0:T(8,128)(2,1)} %denoise.3), channel_id=1, replica_groups=mesh['tm_0'=8,'tm_1'=4,'tm_2'=4,'tensor'=2] {'tm_1','tm_2'}, dimensions={0} | all-to-all | bytes 589824 | tf_op jit(solution)/shard_map/all_to_all | solution.py:501
  106.8 0.0 copy-done.2
  106.8 0.7 plane.3
  107.4 10.3 %all_to_all.23.planes_ref = bf16[8,72,128]{2,1,0:T(8,128)(2,1)S(1)} all-to-all(bf16[8,72,128]{2,1,0:T(8,128)(2,1)S(1)} %get-tuple-element.15), channel_id=1, replica_groups=mesh['tm_0'=8,'tm_1'=4,'tm_2'=4,'tensor'=2] {'tm_0'}, dimensions={0} | all-to-all | bytes 294912 | tf_op jit(solution)/shard_map/all_to_all | solution.py:501
  117.7 0.0 copy-done.3
  117.7 0.7 close.1
  118.4 4.1 %all-gather = f32[144,128]{1,0:T(8,128)S(1)} all-gather(f32[72,128]{1,0:T(8,128)S(1)} %close.1), channel_id=2, replica_groups=mesh['tm_0'=8,'tm_1'=4,'tm_2'=4,'tensor'=2] {'tensor'}, dimensions={0}, use_global_device_ids=true | all-gather | bytes 110592 | tf_op jit(solution)/shard_map/all_gather | solution.py:555
  122.5 0.6 slice_reduce_fusion
  123.1 0.6 slice.8
  (4 shorter events, 0.0 us)
Async XLA Ops:
  0.6 10.7 %collective-permute-start = (bf16[768,1536]{1,0:T(8,128)(2,1)}, bf16[768,1536]{1,0:T(8,128)(2,1)}, u32[]{:S(2)}, u32[]{:S(2)}) collective-permute-start(bf16[768,1536]{1,0:T(8,128)(2,1)} %up_a_hbm.3), channel_id=1, source_target_pairs={{0,1},{1,0},{2,3},{3,2},{4,5},{5,4},{6,7},{7,6},{8,9},{9,8},{10,11... | collective-permute-start | bytes 7077896 | tf_op jit(solution)/shard_map/ppermute | solution.py:523
  3.9 7.9 %collective-permute-start.1 = (bf16[1536,768]{1,0:T(8,128)(2,1)}, bf16[1536,768]{1,0:T(8,128)(2,1)}, u32[]{:S(2)}, u32[]{:S(2)}) collective-permute-start(bf16[1536,768]{1,0:T(8,128)(2,1)} %down_a_hbm.3), channel_id=1, source_target_pairs={{0,1},{1,0},{2,3},{3,2},{4,5},{5,4},{6,7},{7,6},{8,9},{9,8},{10,11... | collective-permute-start | bytes 7077896 | tf_op jit(solution)/shard_map/ppermute | solution.py:524
  11.8 37.2 %copy-start.1 = (s32[4]{0:T(128)S(1)}, s32[4]{0:T(128)}, u32[]{:S(2)}) copy-start(s32[4]{0:T(128)} %pad_add_fusion.where_ref) | copy-start | bytes 52
  11.8 53.9 %copy-start = (f32[1,16384]{1,0:T(1,128)S(1)}, f32[1,16384]{1,0:T(1,128)}, u32[]{:S(2)}) copy-start(f32[1,16384]{1,0:T(1,128)} %param.20) | copy-start | bytes 196612
  70.9 35.9 %copy-start.2 = (s32[4]{0:T(128)S(1)}, s32[4]{0:T(128)}, u32[]{:S(2)}) copy-start(s32[4]{0:T(128)} %pad_add_fusion.where_ref) | copy-start | bytes 52
  70.9 46.9 %copy-start.3 = (f32[2,1]{0,1:T(1,128)S(1)}, f32[2,1]{0,1:T(1,128)}, u32[]{:S(2)}) copy-start(f32[2,1]{0,1:T(1,128)} %param.23) | copy-start | bytes 28
